TPU v7x, 32 devices: a whole 2x2x4 slice. The times are simulated.
32 devices in a mesh: sample: 2 (over x), sy: 4 (over y, core), sz: 4 (over z).
Axes of the slice: x: 2, y: 2, z: 4, core: 2. Of those that a mesh axis runs over, the one named last changes fastest.
Arguments:
- volume: bfloat16 [2, 32, 16, 32, 128], P('sample', None, 'sz', 'sy'), may hold values from -22.5 to 22.5
- amax_history: float32 [4, 16], replicated, may hold values from 0.48 to 2.5
- conv_first: bfloat16 [27, 32, 32], replicated, may hold values from -0.21875 to 0.21875
- conv_second: bfloat16 [27, 32, 32], replicated, may hold values from -0.21875 to 0.21875
- conv_third: bfloat16 [27, 64, 32], P(None, 'sy'), may hold values from -0.21875 to 0.21875
- conv_fourth: bfloat16 [27, 64, 64], P(None, 'sy'), may hold values from -0.15625 to 0.15625
- gain_fine: float32 [2, 32], replicated, may hold values from 0.5 to 1.5
- shift_fine: float32 [2, 32], replicated, may hold values from -0.5 to 0.5
- gain_coarse: float32 [2, 64], P(None, 'sy'), may hold values from 0.5 to 1.5
- shift_coarse: float32 [2, 64], P(None, 'sy'), may hold values from -0.5 to 0.5
Outputs:
- skip_features: bfloat16 [2, 32, 16, 32, 128], P('sample', None, 'sz', 'sy')
- coarse_features: bfloat16 [2, 64, 8, 1024], P('sample', 'sy', 'sz')
- amax_now: float32 [4], replicated
All inputs are finite; a program needn't handle non-finite values.
Results may differ from a plain program's by a relative error of at most 0.012.
Values may be sent and summed in bfloat16 or wider, within the bound.
A program may use at most 128 MiB of HBM per device.

v0:
```python
import functools

import jax
import jax.numpy as jnp
from jax import lax
from jax.experimental import pallas as pl
from jax.experimental.pallas import tpu as pltpu
from jax.sharding import PartitionSpec as P

norm_eps = 1e-05
leak_slope = 0.01
LANES = 128
MESH = pl.DeviceIdType.MESH
F32 = jnp.float32
BF16 = jnp.bfloat16
STEPS = ((-1, 0), (1, 0), (0, -1), (0, 1), (-1, -1), (-1, 1), (1, -1), (1, 1))


def iota(shape, dim):
    return lax.broadcasted_iota(jnp.int32, shape, dim)


def lane_row(column, start):
    n = column.shape[0]
    here = iota((n, LANES), 1) == iota((n, LANES), 0) + start
    return jnp.sum(jnp.where(here, column, 0.0), axis=0, keepdims=True)


def to_column(row, n, start):
    shape = (n, row.shape[1])
    here = iota(shape, 1) == iota(shape, 0) + start
    return jnp.sum(jnp.where(here, row, 0.0), axis=1, keepdims=True)


def leaky(normed):
    return jnp.where(normed >= 0, normed, leak_slope * normed).astype(BF16)


def remote(src, dst, send, recv, where):
    return pltpu.make_async_remote_copy(
        src_ref=src, dst_ref=dst, send_sem=send, recv_sem=recv, device_id=where, device_id_type=MESH
    )


def network(
    sizes,
    volume, hist, c1, c2, c3, c4, gf, sf, gc, sc,
    skip_out, coarse_out, peak_out,
    w1, w2, w3, w4, turn, vol, skip,
    stacked, prod, vals, hid, zface, yface, corner,
    pool, wide3, g3, prod3, vals3, hid3, wide4, g4,
    stat, peak, peak_all,
    halo_s, halo_r, stat_s, stat_r, co_s, co_r, pk_s, pk_r, pa_s, pa_r,
):
    ns, ny, nz = sizes
    zc, yc, ch, xc = vol.shape
    hz, pairs = zc // 2, yc // 4
    tiles = pairs * ny
    oc = c3.shape[1]
    group = ny * nz
    my_s, my_y, my_z = lax.axis_index("sample"), lax.axis_index("sy"), lax.axis_index("sz")
    me = my_y * nz + my_z

    def member(index):
        return {"sy": index // nz, "sz": lax.rem(index, nz)}

    barrier = pltpu.get_barrier_semaphore()
    for k in range(1, group):
        pl.semaphore_signal(barrier, inc=1, device_id=member(lax.rem(me + k, group)), device_id_type=MESH)
    for k in range(1, ns):
        pl.semaphore_signal(
            barrier, inc=1, device_id={"sample": lax.rem(my_s + k, ns)}, device_id_type=MESH
        )

    for matrix, taps in ((w1, c1), (w2, c2), (w3, c3), (w4, c4)):
        out = taps.shape[1]
        for a in range(3):
            parts = [taps[9 * a + k].astype(F32) for k in range(9)]
            matrix[a * out : (a + 1) * out, :] = jnp.concatenate(parts, axis=1).astype(BF16)
    for z in range(zc):
        turn[z] = volume[:, z].astype(F32).reshape(ch * yc, LANES)
    for z in range(zc):
        for y in range(yc):
            vol[z, y] = turn[z, pl.ds(y, ch, yc), :].astype(BF16)
    pl.semaphore_wait(barrier, group - 1 + ns - 1)

    lane = iota((ch, LANES), 1)
    bounds = [jnp.max(hist[l : l + 1, :]) for l in range(4)]

    def inside(dz, dy):
        z, y = my_z + dz, my_y + dy
        return (z >= 0) & (z < nz) & (y >= 0) & (y < ny)

    def landing(layer, d):
        dz, dy = STEPS[d]
        if dy == 0:
            return zface.at[layer, int(dz < 0)]
        if dz == 0:
            return yface.at[layer, int(dy < 0)]
        return corner.at[layer, int(dz < 0) * 2 + int(dy < 0)]

    def halo(src, layer, d):
        dz, dy = STEPS[d]
        zi = 0 if dz < 0 else zc - 1
        yi = 0 if dy < 0 else yc - 1
        if dy == 0:
            src = src.at[zi]
        elif dz == 0:
            src = src.at[:, yi]
        else:
            src = src.at[zi, yi]
        where = {"sy": jnp.clip(my_y + dy, 0, ny - 1), "sz": jnp.clip(my_z + dz, 0, nz - 1)}
        return remote(src, landing(layer, d), halo_s.at[layer, d], halo_r.at[layer, d], where)

    def halo_start(src, layer):
        for d, (dz, dy) in enumerate(STEPS):
            @pl.when(inside(dz, dy))
            def _():
                halo(src, layer, d).start()

            @pl.when(jnp.logical_not(inside(-dz, -dy)))
            def _():
                dst = landing(layer, d)
                dst[...] = jnp.zeros(dst.shape, dst.dtype)

    def halo_wait(src, layer, flat):
        for d, (dz, dy) in enumerate(STEPS):
            if (dz == 0) != flat:
                continue

            @pl.when(inside(-dz, -dy))
            def _():
                halo(src, layer, d).wait_recv()

            @pl.when(inside(dz, dy))
            def _():
                halo(src, layer, d).wait_send()

    def put(zp, yp, values, bound):
        v = jnp.clip(values.astype(F32), -bound, bound)
        left = jnp.where(lane == 0, 0.0, pltpu.roll(v, 1, 1))
        right = jnp.where(lane == LANES - 1, 0.0, pltpu.roll(v, LANES - 1, 1))
        stacked[zp, yp] = jnp.concatenate([left, v, right], axis=0).astype(BF16)

    def put_inner(src, bound):
        def plane(z, top):
            for y in range(yc):
                v = src[z, y]
                top = jnp.maximum(top, jnp.abs(v.astype(F32)))
                put(z + 1, y + 1, v, bound)
            return top

        return jnp.max(lax.fori_loop(0, zc, plane, jnp.zeros((ch, LANES), F32)))

    def put_sides(layer, bound):
        for side in range(2):
            for z in range(zc):
                put(z + 1, side * (yc + 1), yface[layer, side, z], bound)

    def put_ends(layer, bound):
        for side in range(2):
            for y in range(yc):
                put(side * (zc + 1), y + 1, zface[layer, side, y], bound)
            for other in range(2):
                put(side * (zc + 1), other * (yc + 1), corner[layer, side * 2 + other], bound)

    def fine_conv(w, src, layer, bound):
        def plane(zp, carry):
            for y in range(0, yc, 2):
                rows = [stacked[zp, y + i : y + i + 3].reshape(9 * ch, LANES) for i in range(2)]
                prod[zp, y // 2] = jnp.dot(
                    w[...], jnp.concatenate(rows, axis=1), preferred_element_type=F32
                )
            return carry

        halo_wait(src, layer, True)
        put_sides(layer, bound)
        lax.fori_loop(1, zc + 1, plane, 0)
        halo_wait(src, layer, False)
        put_ends(layer, bound)
        lax.fori_loop(0, 2, lambda i, carry: plane(i * (zc + 1), carry), 0)

        def total(z, carry):
            s, q = carry
            for y in range(yc // 2):
                v = (
                    prod[z, y, 0:ch, :]
                    + prod[z + 1, y, ch : 2 * ch, :]
                    + prod[z + 2, y, 2 * ch : 3 * ch, :]
                )
                for i in range(2):
                    part = v[:, i * LANES : (i + 1) * LANES]
                    vals[z, 2 * y + i] = part
                    s, q = s + part, q + part * part
            return s, q

        zero = jnp.zeros((ch, LANES), F32)
        return lax.fori_loop(0, zc, total, (zero, zero))

    def share(buf, row, index, count, send, recv, where):
        buf[index, 0:1, :] = row

        def copy(k, slot):
            other = lax.rem(index + k, count)
            at = index if slot == "mine" else other
            ref = buf.at[at, pl.ds(0, 1)]
            return remote(ref, ref, send.at[k], recv.at[at], where(other))

        for k in sorted(range(1, count), key=lambda k: -min(k % nz, -k % nz)):
            copy(k, "mine").start()
        return copy

    def shared(copy, count):
        for k in range(1, count):
            copy(k, "theirs").wait_recv()
            copy(k, "mine").wait_send()

    def moments(phase, s, q, index, count, where, cells, gain_row, shift_row):
        n = s.shape[0]
        row = lane_row(jnp.sum(s, axis=1, keepdims=True), 0) + lane_row(
            jnp.sum(q, axis=1, keepdims=True), LANES // 2
        )
        buf = stat.at[phase]
        shared(share(buf, row, index, count, stat_s.at[phase], stat_r.at[phase], where), count)
        total = buf[0, 0:1, :]
        for i in range(1, count):
            total = total + buf[i, 0:1, :]
        mean = to_column(total, n, 0) / cells
        spread = to_column(total, n, LANES // 2) / cells - mean * mean
        scaling = lax.rsqrt(spread + norm_eps) * to_column(gain_row, n, 0)
        return mean, scaling, to_column(shift_row, n, 0)

    def fine_act(dst, phase, s, q):
        cells = float(zc * nz * yc * ny * xc)
        mean, scaling, offset = moments(
            phase, s, q, me, group, member, cells, gf[phase : phase + 1, :], sf[phase : phase + 1, :]
        )
        mean, scaling, offset = (jnp.broadcast_to(a, (ch, LANES)) for a in (mean, scaling, offset))

        def plane(z, carry):
            for y in range(yc):
                dst[z, y] = leaky((vals[z, y] - mean) * scaling + offset)
            return carry

        lax.fori_loop(0, zc, plane, 0)

    halo_start(vol, 0)
    peak0 = put_inner(vol, bounds[0])
    s, q = fine_conv(w1, vol, 0, bounds[0])
    fine_act(hid, 0, s, q)
    halo_start(hid, 1)
    peak1 = put_inner(hid, bounds[1])
    s, q = fine_conv(w2, hid, 1, bounds[1])
    fine_act(skip, 1, s, q)

    src_lane, dst_lane = iota((LANES, LANES), 0), iota((LANES, LANES), 1)
    half = LANES // 2
    pick = [
        jnp.where((dst_lane // half == i) & (src_lane == 2 * (dst_lane - i * half)), 1.0, 0.0).astype(BF16)
        for i in range(2)
    ]
    top = jnp.zeros((ch, LANES), F32)
    for z in range(hz):
        for t in range(pairs):
            found = jnp.zeros((ch, LANES), F32)
            for i in range(2):
                y = 4 * t + 2 * i
                block = [skip[2 * z + a, y + b].astype(F32) for a in range(2) for b in range(2)]
                m = jnp.maximum(jnp.maximum(block[0], block[1]), jnp.maximum(block[2], block[3]))
                m = jnp.maximum(m, pltpu.roll(m, LANES - 1, 1))
                found = found + jnp.dot(m.astype(BF16), pick[i], preferred_element_type=F32)
            top = jnp.maximum(top, jnp.abs(found))
            cells = jnp.clip(found, -bounds[2], bounds[2]).astype(BF16)
            pool[z, t] = cells
            g3[z + 1, my_y * pairs + t] = cells
    peak2 = jnp.max(top)

    def coarse_copies(layer, src, block_of, slab_of):
        out = []
        send, recv = co_s.at[layer], co_r.at[layer]
        for k in range(1, ny):
            other = lax.rem(my_y + k, ny)
            out.append((
                True,
                remote(src, slab_of(my_y), send.at[0, k], recv.at[0, my_y], {"sy": other}),
                True,
                remote(src, slab_of(other), send.at[0, k], recv.at[0, other], {"sy": other}),
            ))
        for kind, (step, plane, to) in enumerate(((-1, 0, hz + 1), (1, hz - 1, 0)), start=1):
            z = jnp.clip(my_z + step, 0, nz - 1)
            sends = (my_z + step >= 0) & (my_z + step < nz)
            gets = (my_z - step >= 0) & (my_z - step < nz)
            for y in range(ny):
                where = {"sy": y, "sz": z}
                out.append((
                    sends,
                    remote(src.at[plane], block_of(to, my_y), send.at[kind, y], recv.at[kind, my_y], where),
                    gets,
                    remote(src.at[plane], block_of(to, y), send.at[kind, y], recv.at[kind, y], where),
                ))
        return out

    def guarded(flag, act):
        if flag is True:
            act()
        else:
            pl.when(flag)(act)

    def coarse_start(copies, buf):
        for sends, mine, _, _ in copies:
            guarded(sends, mine.start)
        for at, missing in ((0, my_z == 0), (hz + 1, my_z == nz - 1)):
            @pl.when(missing)
            def _():
                buf[at] = jnp.zeros(buf.shape[1:], buf.dtype)

    def coarse_wait(copies, slab):
        for sends, mine, gets, theirs in copies:
            if (sends is True) != slab:
                continue
            guarded(gets, theirs.wait_recv)
            guarded(sends, mine.wait_send)

    def widen(load, n, wide):
        where = iota((n, LANES), 1)
        column = lax.rem(where, half)
        low = iota((3 * n, LANES), 1) < half

        def plane(z):
            def put3(k, t, v):
                wide[z, k * 3 * n : (k + 1) * 3 * n, t * LANES : (t + 1) * LANES] = v.astype(BF16)

            before = jnp.zeros((3 * n, LANES), F32)
            for t in range(tiles):
                v = load(z, t).astype(F32)
                left = jnp.where(column == 0, 0.0, pltpu.roll(v, 1, 1))
                right = jnp.where(column == half - 1, 0.0, pltpu.roll(v, LANES - 1, 1))
                x = jnp.concatenate([left, v, right], axis=0)
                u = pltpu.roll(x, half, 1)
                put3(1, t, x)
                put3(0, t, jnp.where(low, before, u))
                if t:
                    put3(2, t - 1, jnp.where(low, before, u))
                before = u
            put3(2, tiles - 1, jnp.where(low, before, 0.0))

        return plane

    def coarse_conv(w, wide, load, n, copies):
        widen_plane = widen(load, n, wide)

        def plane(z, carry):
            widen_plane(z)
            prod3[z] = jnp.dot(w[...], wide[z], preferred_element_type=F32)
            return carry

        coarse_wait(copies, True)
        lax.fori_loop(1, hz + 1, plane, 0)
        coarse_wait(copies, False)
        lax.fori_loop(0, 2, lambda i, carry: plane(i * (hz + 1), carry), 0)

    def coarse_sums():
        s = q = jnp.zeros((oc, LANES), F32)
        for z in range(hz):
            for t in range(tiles):
                cols = slice(t * LANES, (t + 1) * LANES)
                v = (
                    prod3[z, 0:oc, cols]
                    + prod3[z + 1, oc : 2 * oc, cols]
                    + prod3[z + 2, 2 * oc : 3 * oc, cols]
                )
                vals3[z, :, cols] = v
                s, q = s + v, q + v * v
        return s, q

    coarse_cells = float(hz * nz * tiles * LANES)

    def slab(index):
        return {"sz": index}

    copies = coarse_copies(
        0,
        pool,
        lambda plane, y: g3.at[plane, pl.ds(y * pairs, pairs)],
        lambda y: g3.at[pl.ds(1, hz), pl.ds(y * pairs, pairs)],
    )
    coarse_start(copies, g3)
    for z in range(zc):
        for y in range(yc):
            turn[z, pl.ds(y, ch, yc), :] = skip[z, y].astype(F32)
    for z in range(zc):
        skip_out[:, z] = turn[z].reshape(ch, yc, LANES).astype(BF16)
    coarse_conv(w3, wide3, lambda z, t: g3[z, t], ch, copies)
    s, q = coarse_sums()
    mean, scaling, offset = moments(2, s, q, my_z, nz, slab, coarse_cells, gc[0:1, :], sc[0:1, :])
    top = jnp.zeros((oc, tiles * LANES), F32)
    for z in range(hz):
        v = leaky((vals3[z] - mean) * scaling + offset).astype(F32)
        top = jnp.maximum(top, jnp.abs(v))
        v = jnp.clip(v, -bounds[3], bounds[3]).astype(BF16)
        hid3[z] = v
        g4[z + 1, my_y] = v
    peak3 = jnp.max(top)
    copies = coarse_copies(
        1, hid3, lambda plane, y: g4.at[plane, y], lambda y: g4.at[pl.ds(1, hz), y]
    )
    coarse_start(copies, g4)

    at = iota((1, LANES), 1)
    row = jnp.zeros((1, LANES), F32)
    for i, value in enumerate((peak0, peak1, peak2, peak3)):
        row = jnp.where(at == i, value, row)
    peaks = share(peak, row, me, group, pk_s, pk_r, member)

    def cells4(z, t):
        return g4[z, :, :, t * LANES : (t + 1) * LANES].reshape(ny * oc, LANES)

    coarse_conv(w4, wide4, cells4, ny * oc, copies)
    shared(peaks, group)
    row = peak[0, 0:1, :]
    for i in range(1, group):
        row = jnp.maximum(row, peak[i, 0:1, :])
    peaks = share(peak_all, row, my_s, ns, pa_s, pa_r, lambda index: {"sample": index})
    s, q = coarse_sums()
    mean, scaling, offset = moments(3, s, q, my_z, nz, slab, coarse_cells, gc[1:2, :], sc[1:2, :])
    for z in range(hz):
        coarse_out[:, z, :] = leaky((vals3[z] - mean) * scaling + offset)
    shared(peaks, ns)
    row = peak_all[0, 0:1, :]
    for i in range(1, ns):
        row = jnp.maximum(row, peak_all[i, 0:1, :])
    for i in range(4):
        peak_out[i] = jnp.max(jnp.where(at == i, row, 0.0))


def per_device(sizes, volume, hist, c1, c2, c3, c4, gf, sf, gc, sc):
    ns, ny, nz = sizes
    _, ch, zc, yc, xc = volume.shape
    oc = c3.shape[1]
    hz, pairs = zc // 2, yc // 4
    tiles = pairs * ny
    flat = tiles * LANES
    assert xc == LANES and zc % 2 == 0 and yc % 4 == 0

    vmem = pl.BlockSpec(memory_space=pltpu.VMEM)
    dma = pltpu.SemaphoreType.DMA
    group = ny * nz
    skip, coarse, peaks = pl.pallas_call(
        functools.partial(network, sizes),
        out_shape=(
            jax.ShapeDtypeStruct((ch, zc, yc, xc), BF16),
            jax.ShapeDtypeStruct((oc, hz, flat), BF16),
            jax.ShapeDtypeStruct((4,), F32),
        ),
        in_specs=[vmem] * 10,
        out_specs=(vmem, vmem, pl.BlockSpec(memory_space=pltpu.SMEM)),
        scratch_shapes=[
            pltpu.VMEM((3 * ch, 9 * ch), BF16),
            pltpu.VMEM((3 * ch, 9 * ch), BF16),
            pltpu.VMEM((3 * oc, 9 * ch), BF16),
            pltpu.VMEM((3 * oc, 9 * oc * ny), BF16),
            pltpu.VMEM((zc, ch * yc, LANES), F32),
            pltpu.VMEM((zc, yc, ch, LANES), BF16),
            pltpu.VMEM((zc, yc, ch, LANES), BF16),
            pltpu.VMEM((zc + 2, yc + 2, 3 * ch, LANES), BF16),
            pltpu.VMEM((zc + 2, yc // 2, 3 * ch, 2 * LANES), F32),
            pltpu.VMEM((zc, yc, ch, LANES), F32),
            pltpu.VMEM((zc, yc, ch, LANES), BF16),
            pltpu.VMEM((2, 2, yc, ch, LANES), BF16),
            pltpu.VMEM((2, 2, zc, ch, LANES), BF16),
            pltpu.VMEM((2, 4, ch, LANES), BF16),
            pltpu.VMEM((hz, pairs, ch, LANES), BF16),
            pltpu.VMEM((hz + 2, 9 * ch, flat), BF16),
            pltpu.VMEM((hz + 2, tiles, ch, LANES), BF16),
            pltpu.VMEM((hz + 2, 3 * oc, flat), F32),
            pltpu.VMEM((hz, oc, flat), F32),
            pltpu.VMEM((hz, oc, flat), BF16),
            pltpu.VMEM((hz + 2, 9 * oc * ny, flat), BF16),
            pltpu.VMEM((hz + 2, ny, oc, flat), BF16),
            pltpu.VMEM((4, group, 8, LANES), F32),
            pltpu.VMEM((group, 8, LANES), F32),
            pltpu.VMEM((ns, 8, LANES), F32),
            dma((2, 8)),
            dma((2, 8)),
            dma((4, group)),
            dma((4, group)),
            dma((2, 3, ny)),
            dma((2, 3, ny)),
            dma((group,)),
            dma((group,)),
            dma((ns,)),
            dma((ns,)),
        ],
        compiler_params=pltpu.CompilerParams(
            collective_id=0, has_side_effects=True, vmem_limit_bytes=56 * 1024 * 1024
        ),
    )(volume[0], hist, c1, c2, c3, c4, gf, sf, gc, sc)
    def finish(a, b, c, oa, ob, oc_):
        oa[...] = a[...]
        ob[...] = b[...]
        for i in range(4):
            oc_[i] = c[i]

    smem = pl.BlockSpec(memory_space=pltpu.SMEM)
    skip, coarse, peaks = pl.pallas_call(
        finish,
        out_shape=tuple(jax.ShapeDtypeStruct(a.shape, a.dtype) for a in (skip, coarse, peaks)),
        in_specs=[vmem, vmem, smem],
        out_specs=(vmem, vmem, smem),
    )(skip, coarse, peaks)
    return skip[None], coarse[None], peaks


def solution(mesh):
    sizes = (mesh.shape["sample"], mesh.shape["sy"], mesh.shape["sz"])
    return jax.shard_map(
        functools.partial(per_device, sizes),
        mesh=mesh,
        in_specs=(
            P("sample", None, "sz", "sy", None),
            P(),
            P(),
            P(),
            P(None, "sy", None),
            P(None, "sy", None),
            P(),
            P(),
            P(None, "sy"),
            P(None, "sy"),
        ),
        out_specs=(P("sample", None, "sz", "sy", None), P("sample", "sy", "sz", None), P()),
        check_vma=False,
    )
```

profile of v0, /device:TPU:0, one launch (start us, length us, event | category | flops | bytes accessed | tf_op | source)
XLA Modules:
  0.0 50.2 jit_solution(30258761913625799)
XLA Ops:
  0.6 47.9 %shard_map.121 = (bf16[32,4,8,128]{3,2,1,0:T(8,128)(2,1)}, bf16[16,2,1024]{2,1,0:T(2,128)(2,1)}, f32[4]{0:T(128)}) custom-call(bf16[32,4,8,128]{3,2,1,0:T(8,128)(2,1)} %bitcast.3, f32[4,16]{1,0:T(4,128)} %hist.1, bf16[27,32,32]{2,1,0:T(8,128)(2,1)} %c1.1, bf16[27,32,32]{2,1,0:T(8,128)(2,1)} %c2.1, bf16[27,16,32]{2,1,0:T(8,128)(2,1)} %c3.1, ...), custom_call_target="tpu_custom_call" | custom-call | tf_op jit(solution)/shard_map/pallas_call | solution.py:448
  48.5 1.7 %shard_map.122 = (bf16[32,4,8,128]{3,2,1,0:T(8,128)(2,1)}, bf16[16,2,1024]{2,1,0:T(2,128)(2,1)}, f32[4]{0:T(128)}) custom-call(bf16[32,4,8,128]{3,2,1,0:T(8,128)(2,1)} %get-tuple-element.9.a, bf16[16,2,1024]{2,1,0:T(2,128)(2,1)} %get-tuple-element.10.b, f32[4]{0:T(128)} %get-tuple-element.11.c), custom_call_target="tpu_custom_call" | custom-call | tf_op jit(solution)/shard_map/pallas_call | solution.py:505
where the time goes:
time: 50.4 us; the launch traced here: 50.2 us
  Pallas kernels  49.6 us (98%)
  between operations  0.64 us (1%)
    pallas_call x1, Pallas kernels, per_device(): pl.pallas_call(functools.partial(network, sizes), out_shape=(jax.ShapeDty...  47.9 us
    pallas_call x1, Pallas kernels, per_device(): pl.pallas_call(finish, out_shape=tuple((jax.ShapeDtypeStruct(a.shape, a.d...  1.71 us

commit v1 on v0

v1 whole, which is shorter than its diff:
```python
import functools

import jax
import jax.numpy as jnp
from jax import lax
from jax.experimental import pallas as pl
from jax.experimental.pallas import tpu as pltpu
from jax.sharding import PartitionSpec as P

norm_eps = 1e-05
leak_slope = 0.01
LANES = 128
HALF = LANES // 2
MESH = pl.DeviceIdType.MESH
F32 = jnp.float32
BF16 = jnp.bfloat16
STEPS = ((-1, 0), (1, 0), (0, -1), (0, 1), (-1, -1), (-1, 1), (1, -1), (1, 1))


def iota(shape, dim):
    return lax.broadcasted_iota(jnp.int32, shape, dim)


def lane_row(column, start):
    n = column.shape[0]
    here = iota((n, LANES), 1) == iota((n, LANES), 0) + start
    return jnp.sum(jnp.where(here, column, 0.0), axis=0, keepdims=True)


def to_column(row, n, start):
    shape = (n, row.shape[1])
    here = iota(shape, 1) == iota(shape, 0) + start
    return jnp.sum(jnp.where(here, row, 0.0), axis=1, keepdims=True)


def remote(src, dst, send, recv, where):
    return pltpu.make_async_remote_copy(
        src_ref=src, dst_ref=dst, send_sem=send, recv_sem=recv, device_id=where, device_id_type=MESH
    )


def rounded(v):
    return v.astype(BF16).astype(F32)


def network(sizes, *refs):
    (
        volume, hist_in, c1_in, c2_in, c3_in, c4_in, gf_in, sf_in, gc_in, sc_in,
        skip_out, coarse_out, peak_out,
        given, hist, c1, c2, c3, c4, gf, sf, gc, sc,
        w1, w2, w3, w4, grow, turn, vol, vals1, vals2, stacked, prod,
        pool, vals3, vals4, fin, wide3, wide4, prod3,
        zf0, yf0, co0, zf1, yf1, co1, zf2, yf2, co2, zf3, yf3, co3,
        stat, peak_all,
        in_s, halo_s, halo_r, stat_s, stat_r, w_s, w_r, fin_s, fin_r, pa_s, pa_r,
    ) = refs
    ns, ny, nz = sizes
    zc, yc, ch, xc = vol.shape
    hz, pairs = zc // 2, yc // 4
    oc = c3.shape[1]
    wc = ny * oc
    group = ny * nz
    my_s, my_y, my_z = lax.axis_index("sample"), lax.axis_index("sy"), lax.axis_index("sz")
    me = my_y * nz + my_z

    def member(index):
        return {"sy": index // nz, "sz": lax.rem(index, nz)}

    barrier = pltpu.get_barrier_semaphore()
    for k in range(1, group):
        pl.semaphore_signal(barrier, inc=1, device_id=member(lax.rem(me + k, group)), device_id_type=MESH)
    for k in range(1, ns):
        pl.semaphore_signal(
            barrier, inc=1, device_id={"sample": lax.rem(my_s + k, ns)}, device_id_type=MESH
        )

    pairs_in = (
        (volume, given), (hist_in, hist), (c1_in, c1), (c2_in, c2), (c3_in, c3), (c4_in, c4),
        (gf_in, gf), (sf_in, sf), (gc_in, gc), (sc_in, sc),
    )
    fetch = [pltpu.make_async_copy(a, b, in_s.at[i]) for i, (a, b) in enumerate(pairs_in)]
    for copy in fetch:
        copy.start()

    def inside(dz, dy):
        z, y = my_z + dz, my_y + dy
        return (z >= 0) & (z < nz) & (y >= 0) & (y < ny)

    class Halo:
        def __init__(self, layer, src, zface, yface, corner):
            self.layer, self.src = layer, src
            self.zface, self.yface, self.corner = zface, yface, corner

        def landing(self, d):
            dz, dy = STEPS[d]
            if dy == 0:
                return self.zface.at[int(dz < 0)]
            if dz == 0:
                return self.yface.at[int(dy < 0)]
            return self.corner.at[int(dz < 0) * 2 + int(dy < 0)]

        def copy(self, d):
            dz, dy = STEPS[d]
            planes, rows = self.src.shape[0], self.src.shape[1]
            zi = 0 if dz < 0 else planes - 1
            yi = 0 if dy < 0 else rows - 1
            if dy == 0:
                src = self.src.at[zi]
            elif dz == 0:
                src = self.src.at[:, yi]
            else:
                src = self.src.at[zi, yi]
            where = {"sy": jnp.clip(my_y + dy, 0, ny - 1), "sz": jnp.clip(my_z + dz, 0, nz - 1)}
            at = self.layer, d
            return remote(src, self.landing(d), halo_s.at[at], halo_r.at[at], where)

        def start(self):
            for d, (dz, dy) in enumerate(STEPS):
                @pl.when(inside(dz, dy))
                def _():
                    self.copy(d).start()

        def blank(self):
            for d, (dz, dy) in enumerate(STEPS):
                @pl.when(jnp.logical_not(inside(-dz, -dy)))
                def _():
                    dst = self.landing(d)
                    dst[...] = jnp.zeros(dst.shape, dst.dtype)

        def wait(self, flat):
            for d, (dz, dy) in enumerate(STEPS):
                if (dz == 0) != flat:
                    continue

                @pl.when(inside(-dz, -dy))
                def _():
                    self.copy(d).wait_recv()

                @pl.when(inside(dz, dy))
                def _():
                    self.copy(d).wait_send()

    halo0 = Halo(0, vol, zf0, yf0, co0)
    halo1 = Halo(1, vals1, zf1, yf1, co1)
    halo2 = Halo(2, pool, zf2, yf2, co2)
    halo3 = Halo(3, vals3, zf3, yf3, co3)

    fetch[0].wait()
    for z in range(zc):
        turn[z] = given[:, z].astype(F32).reshape(ch * yc, LANES)
    for z in range(zc):
        for y in range(yc):
            vol[z, y] = turn[z, pl.ds(y, ch, yc), :].astype(BF16)
    pl.semaphore_wait(barrier, group - 1 + ns - 1)
    halo0.start()
    for copy in fetch[1:]:
        copy.wait()

    bounds = [jnp.max(hist[l : l + 1, :]) for l in range(4)]
    lane = iota((ch, LANES), 1)

    def limit(layer, dz, dy):
        if dz == 0 and dy == 0:
            return bounds[layer]
        return jnp.where(inside(dz, dy), bounds[layer], 0.0)

    def put(zp, yp, v, bound):
        v = jnp.clip(v, -bound, bound)
        left = jnp.where(lane == 0, 0.0, pltpu.roll(v, 1, 1))
        right = jnp.where(lane == LANES - 1, 0.0, pltpu.roll(v, LANES - 1, 1))
        stacked[zp, yp] = jnp.concatenate([left, v, right], axis=0).astype(BF16)

    def fine_inner(src, value, layer):
        def plane(z, top):
            for y in range(yc):
                v = value(src[z, y])
                top = jnp.maximum(top, jnp.abs(v))
                put(z + 1, y + 1, v, bounds[layer])
            return top

        top = lax.fori_loop(0, zc, plane, jnp.zeros((ch, LANES), F32))
        return jnp.max(rounded(top))

    def fine_conv(w, halo, value, layer, out):
        def plane(zp, carry):
            for y in range(0, yc, 2):
                rows = [stacked[zp, y + i : y + i + 3].reshape(9 * ch, LANES) for i in range(2)]
                prod[zp, y // 2] = jnp.dot(
                    w[...], jnp.concatenate(rows, axis=1), preferred_element_type=F32
                )
            return carry

        halo.wait(True)
        for side in range(2):
            bound = limit(layer, 0, 2 * side - 1)
            for z in range(zc):
                put(z + 1, side * (yc + 1), value(halo.yface[side, z]), bound)
        lax.fori_loop(1, zc + 1, plane, 0)
        halo.wait(False)
        for side in range(2):
            bound = limit(layer, 2 * side - 1, 0)
            for y in range(yc):
                put(side * (zc + 1), y + 1, value(halo.zface[side, y]), bound)
            for other in range(2):
                bound = limit(layer, 2 * side - 1, 2 * other - 1)
                put(side * (zc + 1), other * (yc + 1), value(halo.corner[side * 2 + other]), bound)
        lax.fori_loop(0, 2, lambda i, carry: plane(i * (zc + 1), carry), 0)

        def total(z, carry):
            s, q = carry
            for y in range(yc // 2):
                v = (
                    prod[z, y, 0:ch, :]
                    + prod[z + 1, y, ch : 2 * ch, :]
                    + prod[z + 2, y, 2 * ch : 3 * ch, :]
                )
                for i in range(2):
                    part = v[:, i * LANES : (i + 1) * LANES]
                    out[z, 2 * y + i] = part
                    s, q = s + part, q + part * part
            return s, q

        zero = jnp.zeros((ch, LANES), F32)
        return lax.fori_loop(0, zc, total, (zero, zero))

    class Stats:
        def __init__(self, phase, rows):
            self.phase, self.count = phase, len(rows)
            for r, row in enumerate(rows):
                stat[phase, me, r : r + 1, :] = row
            for k in sorted(range(1, group), key=lambda k: -min(k % nz, -k % nz)):
                self.copy(k, True).start()

        def copy(self, k, mine):
            other = lax.rem(me + k, group)
            at = me if mine else other
            ref = stat.at[self.phase, at, pl.ds(0, self.count)]
            sems = stat_s.at[self.phase, k], stat_r.at[self.phase, at]
            return remote(ref, ref, *sems, member(other))

        def wait(self):
            for k in range(1, group):
                self.copy(k, False).wait_recv()
                self.copy(k, True).wait_send()

        def rows(self, r):
            return [stat[self.phase, i, r : r + 1, :] for i in range(group)]

    def tree(op, parts):
        while len(parts) > 1:
            parts = [op(*parts[i : i + 2]) if i + 1 < len(parts) else parts[i] for i in range(0, len(parts), 2)]
        return parts[0]

    def sums_row(s, q):
        return lane_row(jnp.sum(s, axis=1, keepdims=True), 0) + lane_row(
            jnp.sum(q, axis=1, keepdims=True), HALF
        )

    def norm_of(total, n, start, cells, gain, shift):
        mean = to_column(total, n, start) / cells
        spread = to_column(total, n, start + HALF) / cells - mean * mean
        scaling = lax.rsqrt(spread + norm_eps) * gain
        return mean, scaling, shift

    def act_of(norm, wide=True):
        n = norm[0].shape[0]
        mean, scaling, offset = (
            tuple(jnp.broadcast_to(a, (n, LANES)) for a in norm) if wide else norm
        )

        def act(v):
            normed = (v - mean) * scaling + offset
            return jnp.maximum(normed, leak_slope * normed)

        return act

    def build(dst, taps):
        out = taps.shape[1]
        for a in range(3):
            parts = [taps[9 * a + k].astype(F32) for k in range(9)]
            dst[a * out : (a + 1) * out, :] = jnp.concatenate(parts, axis=1).astype(BF16)

    def plain(v):
        return v.astype(F32)

    build(w1, c1)
    halo0.blank()
    peak0 = fine_inner(vol, plain, 0)
    build(w2, c2)
    build(w3.at[my_y], c3)
    build(w4.at[my_y], c4)
    own_gain = to_column(gc[0:1, :], oc, 0)
    own_shift = to_column(sc[0:1, :], oc, 0)
    grow[my_y, 0:1, :] = lane_row(own_gain, my_y * oc) + lane_row(own_shift, HALF + my_y * oc)
    for halo in (halo1, halo2, halo3):
        halo.blank()
    s, q = fine_conv(w1, halo0, plain, 0, vals1)
    stats = Stats(0, [sums_row(s, q)])
    halo1.start()

    def gathers(mine):
        out = []
        for k in range(1, ny):
            other = lax.rem(my_y + k, ny)
            at = my_y if mine else other
            for i, buf in enumerate((grow, w3, w4)):
                out.append(remote(buf.at[at], buf.at[at], w_s.at[i, k], w_r.at[i, at], {"sy": other}))
        return out

    for copy in gathers(True):
        copy.start()
    fine_cells = float(zc * nz * yc * ny * xc)

    def fine_norm(layer):
        total = tree(jnp.add, stats.rows(0))
        gain, shift = to_column(gf[layer : layer + 1, :], ch, 0), to_column(sf[layer : layer + 1, :], ch, 0)
        return norm_of(total, ch, 0, fine_cells, gain, shift)

    stats.wait()
    act = act_of(fine_norm(0))

    peak1 = fine_inner(vals1, act, 1)
    s, q = fine_conv(w2, halo1, act, 1, vals2)
    stats = Stats(1, [sums_row(s, q)])

    pick = jnp.where(iota((2 * LANES, LANES), 0) == 2 * iota((2 * LANES, LANES), 1), 1.0, 0.0).astype(BF16)
    for z in range(hz):
        for t in range(pairs):
            found = []
            for i in range(2):
                y = 4 * t + 2 * i
                block = [vals2[2 * z + a, y + b] for a in range(2) for b in range(2)]
                m = tree(jnp.maximum, block)
                found.append(jnp.maximum(m, pltpu.roll(m, LANES - 1, 1)))
            m = jnp.concatenate(found, axis=1)
            high = rounded(m)
            middle = rounded(m - high)
            low = m - high - middle
            split = jnp.concatenate([high, middle, low], axis=0).astype(BF16)
            r = jnp.dot(split, pick, preferred_element_type=F32)
            pool[z, t] = r[0:ch] + r[ch : 2 * ch] + r[2 * ch : 3 * ch]
    halo2.start()
    for mine, theirs in zip(gathers(True), gathers(False)):
        theirs.wait_recv()
        mine.wait_send()
    stats.wait()
    act_skip = act_of(fine_norm(1))

    def widen(n, zp, load, wide):
        where = iota((n, LANES), 1)
        column = lax.rem(where, HALF)
        below = iota((3 * n, LANES), 1) < HALF
        xs, us = [], []
        for tp in range(pairs + 2):
            v = load(tp)
            left = jnp.where(column == 0, 0.0, pltpu.roll(v, 1, 1))
            right = jnp.where(column == HALF - 1, 0.0, pltpu.roll(v, LANES - 1, 1))
            x = jnp.concatenate([left, v, right], axis=0)
            xs.append(x)
            us.append(pltpu.roll(x, HALF, 1))
        for t in range(pairs):
            cols = slice(t * LANES, (t + 1) * LANES)
            rows = (
                jnp.where(below, us[t], us[t + 1]), xs[t + 1], jnp.where(below, us[t + 1], us[t + 2])
            )
            for b, part in enumerate(rows):
                wide[zp, b * 3 * n : (b + 1) * 3 * n, cols] = part.astype(BF16)

    def coarse_conv(w, n, halo, act, layer, wide, store):
        top = jnp.zeros((n, LANES), F32)

        def inner(zp):
            def load(tp):
                nonlocal top
                if tp in (0, pairs + 1):
                    side = int(tp > 0)
                    bound = limit(layer, 0, 2 * side - 1)
                    v = act(halo.yface[side, zp - 1])
                else:
                    bound = bounds[layer]
                    v = act(halo.src[zp - 1, tp - 1])
                    top = jnp.maximum(top, jnp.abs(v))
                return jnp.clip(v, -bound, bound)

            return load

        def outer(side):
            def load(tp):
                if tp in (0, pairs + 1):
                    other = int(tp > 0)
                    bound = limit(layer, 2 * side - 1, 2 * other - 1)
                    v = act(halo.corner[side * 2 + other])
                else:
                    bound = limit(layer, 2 * side - 1, 0)
                    v = act(halo.zface[side, tp - 1])
                return jnp.clip(v, -bound, bound)

            return load

        def plane(zp, load):
            widen(n, zp, load, wide)
            weights = w[...].reshape(3 * wc, 9 * n)
            prod3[zp] = jnp.dot(weights, wide[zp], preferred_element_type=F32)

        halo.wait(True)
        for zp in range(1, hz + 1):
            plane(zp, inner(zp))
        halo.wait(False)
        for side in range(2):
            plane(side * (hz + 1), outer(side))

        parts = []
        for y in range(ny):
            base = 3 * oc * y
            s = q = jnp.zeros((oc, LANES), F32)
            most = least = None
            for z in range(hz):
                for t in range(pairs):
                    cols = slice(t * LANES, (t + 1) * LANES)
                    v = (
                        prod3[z, base : base + oc, cols]
                        + prod3[z + 1, base + oc : base + 2 * oc, cols]
                        + prod3[z + 2, base + 2 * oc : base + 3 * oc, cols]
                    )
                    store(y, z, t, v)
                    s, q = s + v, q + v * v
                    most = v if most is None else jnp.maximum(most, v)
                    least = -v if least is None else jnp.maximum(least, -v)
            parts.append((s, q, most, least))
        joined = [jnp.concatenate(list(p), axis=0) for p in zip(*parts)]
        return joined, jnp.max(rounded(top))

    def store3(y, z, t, v):
        vals3[z, t, y * oc : (y + 1) * oc, :] = v

    def store4(y, z, t, v):
        vals4[y, z, t] = v

    (s, q, most, least), peak2 = coarse_conv(w3, ch, halo2, act_skip, 2, wide3, store3)
    at = iota((1, LANES), 1)
    row = jnp.zeros((1, LANES), F32)
    for i, value in enumerate((peak0, peak1, peak2)):
        row = jnp.where(at == i, value, row)
    ends = lane_row(jnp.max(most, axis=1, keepdims=True), 0) + lane_row(
        jnp.max(least, axis=1, keepdims=True), HALF
    )
    stats = Stats(2, [sums_row(s, q), ends, row])
    halo3.start()

    for z in range(zc):
        for y in range(yc):
            turn[z, pl.ds(y, ch, yc), :] = act_skip(vals2[z, y])
    for z in range(zc):
        skip_out[:, z] = turn[z].reshape(ch, yc, LANES).astype(BF16)

    coarse_cells = float(hz * nz * pairs * ny * LANES)
    gains = tree(jnp.add, [grow[y, 0:1, :] for y in range(ny)])
    stats.wait()
    third = stats
    total = tree(jnp.add, third.rows(0))
    norm3 = norm_of(total, wc, 0, coarse_cells, to_column(gains, wc, 0), to_column(gains, wc, HALF))
    (s, q, _, _), _ = coarse_conv(w4, wc, halo3, act_of(norm3), 3, wide4, store4)
    stats = Stats(3, [sums_row(s, q)])

    def blocks(mine):
        out = []
        for k in range(1, ny):
            other = lax.rem(my_y + k, ny)
            at = my_y if mine else other
            out.append(remote(vals4.at[other], fin.at[at], fin_s.at[k], fin_r.at[at], {"sy": other}))
        return out

    for copy in blocks(True):
        copy.start()
    fin[my_y] = vals4[my_y]

    ends = tree(jnp.maximum, third.rows(1))
    act = act_of(norm3, False)
    high, low = act(to_column(ends, wc, 0)), act(-to_column(ends, wc, HALF))
    peak3 = jnp.max(rounded(jnp.maximum(jnp.abs(high), jnp.abs(low))))
    row = jnp.where(at == 3, peak3, tree(jnp.maximum, third.rows(2)))
    peak_all[my_s, 0:1, :] = row

    def across(k, mine):
        other = lax.rem(my_s + k, ns)
        slot = my_s if mine else other
        ref = peak_all.at[slot, pl.ds(0, 1)]
        return remote(ref, ref, pa_s.at[k], pa_r.at[slot], {"sample": other})

    for k in range(1, ns):
        across(k, True).start()

    own_gain = to_column(gc[1:2, :], oc, 0)
    own_shift = to_column(sc[1:2, :], oc, 0)
    for mine, theirs in zip(blocks(True), blocks(False)):
        theirs.wait_recv()
        mine.wait_send()
    stats.wait()
    total = tree(jnp.add, stats.rows(0))
    act = act_of(norm_of(total, oc, my_y * oc, coarse_cells, own_gain, own_shift))
    for z in range(hz):
        cells = [act(fin[y, z, t]) for y in range(ny) for t in range(pairs)]
        coarse_out[:, z, :] = jnp.concatenate(cells, axis=1).astype(BF16)

    for k in range(1, ns):
        across(k, False).wait_recv()
        across(k, True).wait_send()
    row = tree(jnp.maximum, [peak_all[i, 0:1, :] for i in range(ns)])
    for i in range(4):
        peak_out[i] = jnp.max(jnp.where(at == i, row, 0.0))


def per_device(sizes, volume, hist, c1, c2, c3, c4, gf, sf, gc, sc):
    ns, ny, nz = sizes
    _, ch, zc, yc, xc = volume.shape
    oc = c3.shape[1]
    wc = ny * oc
    hz, pairs = zc // 2, yc // 4
    flat = pairs * ny * LANES
    group = ny * nz
    assert xc == LANES and zc % 2 == 0 and yc % 4 == 0 and wc <= HALF

    args = (volume[0], hist, c1, c2, c3, c4, gf, sf, gc, sc)
    vmem = pl.BlockSpec(memory_space=pltpu.VMEM)
    dma = pltpu.SemaphoreType.DMA

    def faces(planes, rows, n, dtype):
        return [
            pltpu.VMEM((2, rows, n, LANES), dtype),
            pltpu.VMEM((2, planes, n, LANES), dtype),
            pltpu.VMEM((4, n, LANES), dtype),
        ]

    skip, coarse, peaks = pl.pallas_call(
        functools.partial(network, sizes),
        out_shape=(
            jax.ShapeDtypeStruct((ch, zc, yc, xc), BF16),
            jax.ShapeDtypeStruct((oc, hz, flat), BF16),
            jax.ShapeDtypeStruct((4,), F32),
        ),
        in_specs=[pl.BlockSpec(memory_space=IN_SPACE)] * len(args),
        out_specs=(vmem, vmem, pl.BlockSpec(memory_space=pltpu.SMEM)),
        scratch_shapes=[
            *[pltpu.VMEM(a.shape, a.dtype) for a in args],
            pltpu.VMEM((3 * ch, 9 * ch), BF16),
            pltpu.VMEM((3 * ch, 9 * ch), BF16),
            pltpu.VMEM((ny, 3 * oc, 9 * ch), BF16),
            pltpu.VMEM((ny, 3 * oc, 9 * wc), BF16),
            pltpu.VMEM((ny, 8, LANES), F32),
            pltpu.VMEM((zc, ch * yc, LANES), F32),
            pltpu.VMEM((zc, yc, ch, LANES), BF16),
            pltpu.VMEM((zc, yc, ch, LANES), F32),
            pltpu.VMEM((zc, yc, ch, LANES), F32),
            pltpu.VMEM((zc + 2, yc + 2, 3 * ch, LANES), BF16),
            pltpu.VMEM((zc + 2, yc // 2, 3 * ch, 2 * LANES), F32),
            pltpu.VMEM((hz, pairs, ch, LANES), F32),
            pltpu.VMEM((hz, pairs, wc, LANES), F32),
            pltpu.VMEM((ny, hz, pairs, oc, LANES), F32),
            pltpu.VMEM((ny, hz, pairs, oc, LANES), F32),
            pltpu.VMEM((hz + 2, 9 * ch, pairs * LANES), BF16),
            pltpu.VMEM((hz + 2, 9 * wc, pairs * LANES), BF16),
            pltpu.VMEM((hz + 2, 3 * wc, pairs * LANES), F32),
            *faces(zc, yc, ch, BF16),
            *faces(zc, yc, ch, F32),
            *faces(hz, pairs, ch, F32),
            *faces(hz, pairs, wc, F32),
            pltpu.VMEM((4, group, 8, LANES), F32),
            pltpu.VMEM((ns, 8, LANES), F32),
            dma((len(args),)),
            dma((4, 8)),
            dma((4, 8)),
            dma((4, group)),
            dma((4, group)),
            dma((3, ny)),
            dma((3, ny)),
            dma((ny,)),
            dma((ny,)),
            dma((ns,)),
            dma((ns,)),
        ],
        compiler_params=pltpu.CompilerParams(
            collective_id=0, has_side_effects=True, vmem_limit_bytes=VMEM_BYTES
        ),
    )(*args)

    def finish(a, b, c, oa, ob, oc_):
        oa[...] = a[...]
        ob[...] = b[...]
        for i in range(4):
            oc_[i] = c[i]

    smem = pl.BlockSpec(memory_space=pltpu.SMEM)
    skip, coarse, peaks = pl.pallas_call(
        finish,
        out_shape=tuple(jax.ShapeDtypeStruct(a.shape, a.dtype) for a in (skip, coarse, peaks)),
        in_specs=[vmem, vmem, smem],
        out_specs=(vmem, vmem, smem),
        compiler_params=pltpu.CompilerParams(vmem_limit_bytes=FINISH_BYTES),
    )(skip, coarse, peaks)
    return skip[None], coarse[None], peaks


IN_SPACE = pltpu.HBM
VMEM_BYTES = 56 * 1024 * 1024
FINISH_BYTES = 56 * 1024 * 1024


def solution(mesh):
    sizes = (mesh.shape["sample"], mesh.shape["sy"], mesh.shape["sz"])
    return jax.shard_map(
        functools.partial(per_device, sizes),
        mesh=mesh,
        in_specs=(
            P("sample", None, "sz", "sy", None),
            P(),
            P(),
            P(),
            P(None, "sy", None),
            P(None, "sy", None),
            P(),
            P(),
            P(None, "sy"),
            P(None, "sy"),
        ),
        out_specs=(P("sample", None, "sz", "sy", None), P("sample", "sy", "sz", None), P()),
        check_vma=False,
    )
```

time: 50.4 us -> 38.1 us (0.76)
  Pallas kernels: 49.6 us -> 37.3 us
    pallas_call x1, Pallas kernels: 47.9 us -> 35.6 us  [per_device(): pl.pallas_call(functools.partial(network, sizes), out_shape=(jax.ShapeDty...]
where the time goes in v1:
time: 38.1 us; the launch traced here: 38 us
  Pallas kernels  37.3 us (98%)
  between operations  0.64 us (2%)
    pallas_call x1, Pallas kernels, per_device(): pl.pallas_call(functools.partial(network, sizes), out_shape=(jax.ShapeDty...  35.6 us
    pallas_call x1, Pallas kernels, per_device(): pl.pallas_call(finish, out_shape=tuple((jax.ShapeDtypeStruct(a.shape, a.d...  1.71 us

profile of v1, /device:TPU:0, one launch (start us, length us, event | category | flops | bytes accessed | tf_op | source)
XLA Modules:
  0.0 38.0 jit_solution(5665720521882067487)
XLA Ops:
  0.6 35.6 %shard_map.121 = (bf16[32,4,8,128]{3,2,1,0:T(8,128)(2,1)}, bf16[16,2,1024]{2,1,0:T(2,128)(2,1)}, f32[4]{0:T(128)}) custom-call(bf16[32,4,8,128]{3,2,1,0:T(8,128)(2,1)} %bitcast.3, f32[4,16]{1,0:T(4,128)} %refs_1_.1, bf16[27,32,32]{2,1,0:T(8,128)(2,1)} %refs_2_.1, bf16[27,32,32]{2,1,0:T(8,128)(2,1)} %refs_3_.1, bf16[27,16,32]{2,1,0:T(8,128)(2,1)} %refs_4_.1, ...), custom_call_target="tpu_custom_call" | custom-call | tf_op jit(solution)/shard_map/pallas_call | solution.py:534
  36.3 1.7 %shard_map.122 = (bf16[32,4,8,128]{3,2,1,0:T(8,128)(2,1)}, bf16[16,2,1024]{2,1,0:T(2,128)(2,1)}, f32[4]{0:T(128)}) custom-call(bf16[32,4,8,128]{3,2,1,0:T(8,128)(2,1)} %get-tuple-element.9.a, bf16[16,2,1024]{2,1,0:T(2,128)(2,1)} %get-tuple-element.10.b, f32[4]{0:T(128)} %get-tuple-element.11.c), custom_call_target="tpu_custom_call" | custom-call | tf_op jit(solution)/shard_map/pallas_call | solution.py:593

commit v2 on v1

--- a/solution.py
+++ b/solution.py
@@ -63,17 +63,6 @@
     my_s, my_y, my_z = lax.axis_index("sample"), lax.axis_index("sy"), lax.axis_index("sz")
     me = my_y * nz + my_z
 
-    def member(index):
-        return {"sy": index // nz, "sz": lax.rem(index, nz)}
-
-    barrier = pltpu.get_barrier_semaphore()
-    for k in range(1, group):
-        pl.semaphore_signal(barrier, inc=1, device_id=member(lax.rem(me + k, group)), device_id_type=MESH)
-    for k in range(1, ns):
-        pl.semaphore_signal(
-            barrier, inc=1, device_id={"sample": lax.rem(my_s + k, ns)}, device_id_type=MESH
-        )
-
     pairs_in = (
         (volume, given), (hist_in, hist), (c1_in, c1), (c2_in, c2), (c3_in, c3), (c4_in, c4),
         (gf_in, gf), (sf_in, sf), (gc_in, gc), (sc_in, sc),
@@ -81,6 +70,28 @@
     fetch = [pltpu.make_async_copy(a, b, in_s.at[i]) for i, (a, b) in enumerate(pairs_in)]
     for copy in fetch:
         copy.start()
+
+    def ahead(index, k, count):
+        index = index + k
+        return jnp.where(index >= count, index - count, index)
+
+    ys = [my_y] + [ahead(my_y, k, ny) for k in range(1, ny)]
+    zs = [my_z] + [ahead(my_z, k, nz) for k in range(1, nz)]
+    far = sorted(range(1, group), key=lambda k: -min(k % nz, -k % nz))
+
+    def member(k):
+        return {"sy": ys[k // nz], "sz": zs[k % nz]}
+
+    def slot_of(k):
+        return ys[k // nz] * nz + zs[k % nz]
+
+    barrier = pltpu.get_barrier_semaphore()
+    for k in far:
+        pl.semaphore_signal(barrier, inc=1, device_id=member(k), device_id_type=MESH)
+    for k in range(1, ns):
+        pl.semaphore_signal(
+            barrier, inc=1, device_id={"sample": ahead(my_s, k, ns)}, device_id_type=MESH
+        )
 
     def inside(dz, dy):
         z, y = my_z + dz, my_y + dy
@@ -178,24 +189,45 @@
                 put(z + 1, y + 1, v, bounds[layer])
             return top
 
-        top = lax.fori_loop(0, zc, plane, jnp.zeros((ch, LANES), F32))
+        top = lax.fori_loop(0, zc, plane, jnp.zeros((ch, LANES), F32), unroll=True)
         return jnp.max(rounded(top))
 
     def fine_conv(w, halo, value, layer, out):
-        def plane(zp, carry):
-            for y in range(0, yc, 2):
-                rows = [stacked[zp, y + i : y + i + 3].reshape(9 * ch, LANES) for i in range(2)]
-                prod[zp, y // 2] = jnp.dot(
+        half = yc // 2
+
+        def tiles(zp, found):
+            for t in found:
+                rows = [stacked[zp, y : y + 3].reshape(9 * ch, LANES) for y in (2 * t, 2 * t + 1)]
+                prod[zp, t] = jnp.dot(
                     w[...], jnp.concatenate(rows, axis=1), preferred_element_type=F32
                 )
-            return carry
-
+
+        def total(z, carry):
+            s, q = carry
+            for t in range(half):
+                v = (
+                    prod[z, t, 0:ch, :]
+                    + prod[z + 1, t, ch : 2 * ch, :]
+                    + prod[z + 2, t, 2 * ch : 3 * ch, :]
+                )
+                for i in range(2):
+                    part = v[:, i * LANES : (i + 1) * LANES]
+                    out[z, 2 * t + i] = part
+                    s, q = s + part, q + part * part
+            return s, q
+
+        for zp in range(1, zc + 1):
+            tiles(zp, range(1, half - 1))
         halo.wait(True)
         for side in range(2):
             bound = limit(layer, 0, 2 * side - 1)
             for z in range(zc):
                 put(z + 1, side * (yc + 1), value(halo.yface[side, z]), bound)
-        lax.fori_loop(1, zc + 1, plane, 0)
+        for zp in range(1, zc + 1):
+            tiles(zp, (0, half - 1))
+        carry = jnp.zeros((ch, LANES), F32), jnp.zeros((ch, LANES), F32)
+        for z in range(1, zc - 1):
+            carry = total(z, carry)
         halo.wait(False)
         for side in range(2):
             bound = limit(layer, 2 * side - 1, 0)
@@ -204,39 +236,24 @@
             for other in range(2):
                 bound = limit(layer, 2 * side - 1, 2 * other - 1)
                 put(side * (zc + 1), other * (yc + 1), value(halo.corner[side * 2 + other]), bound)
-        lax.fori_loop(0, 2, lambda i, carry: plane(i * (zc + 1), carry), 0)
-
-        def total(z, carry):
-            s, q = carry
-            for y in range(yc // 2):
-                v = (
-                    prod[z, y, 0:ch, :]
-                    + prod[z + 1, y, ch : 2 * ch, :]
-                    + prod[z + 2, y, 2 * ch : 3 * ch, :]
-                )
-                for i in range(2):
-                    part = v[:, i * LANES : (i + 1) * LANES]
-                    out[z, 2 * y + i] = part
-                    s, q = s + part, q + part * part
-            return s, q
-
-        zero = jnp.zeros((ch, LANES), F32)
-        return lax.fori_loop(0, zc, total, (zero, zero))
+            tiles(side * (zc + 1), range(half))
+        for z in (0, zc - 1):
+            carry = total(z, carry)
+        return carry
 
     class Stats:
         def __init__(self, phase, rows):
             self.phase, self.count = phase, len(rows)
             for r, row in enumerate(rows):
                 stat[phase, me, r : r + 1, :] = row
-            for k in sorted(range(1, group), key=lambda k: -min(k % nz, -k % nz)):
+            for k in far:
                 self.copy(k, True).start()
 
         def copy(self, k, mine):
-            other = lax.rem(me + k, group)
-            at = me if mine else other
+            at = me if mine else slot_of(k)
             ref = stat.at[self.phase, at, pl.ds(0, self.count)]
             sems = stat_s.at[self.phase, k], stat_r.at[self.phase, at]
-            return remote(ref, ref, *sems, member(other))
+            return remote(ref, ref, *sems, member(k))
 
         def wait(self):
             for k in range(1, group):
@@ -268,8 +285,8 @@
             tuple(jnp.broadcast_to(a, (n, LANES)) for a in norm) if wide else norm
         )
 
-        def act(v):
-            normed = (v - mean) * scaling + offset
+        def act(v, rows=slice(None)):
+            normed = (v - mean[rows]) * scaling[rows] + offset[rows]
             return jnp.maximum(normed, leak_slope * normed)
 
         return act
@@ -301,7 +318,7 @@
     def gathers(mine):
         out = []
         for k in range(1, ny):
-            other = lax.rem(my_y + k, ny)
+            other = ys[k]
             at = my_y if mine else other
             for i, buf in enumerate((grow, w3, w4)):
                 out.append(remote(buf.at[at], buf.at[at], w_s.at[i, k], w_r.at[i, at], {"sy": other}))
@@ -347,52 +364,57 @@
     act_skip = act_of(fine_norm(1))
 
     def widen(n, zp, load, wide):
-        where = iota((n, LANES), 1)
+        part = 2 * 8
+        where = iota((part, LANES), 1)
         column = lax.rem(where, HALF)
-        below = iota((3 * n, LANES), 1) < HALF
-        xs, us = [], []
-        for tp in range(pairs + 2):
-            v = load(tp)
-            left = jnp.where(column == 0, 0.0, pltpu.roll(v, 1, 1))
-            right = jnp.where(column == HALF - 1, 0.0, pltpu.roll(v, LANES - 1, 1))
-            x = jnp.concatenate([left, v, right], axis=0)
-            xs.append(x)
-            us.append(pltpu.roll(x, HALF, 1))
-        for t in range(pairs):
-            cols = slice(t * LANES, (t + 1) * LANES)
-            rows = (
-                jnp.where(below, us[t], us[t + 1]), xs[t + 1], jnp.where(below, us[t + 1], us[t + 2])
-            )
-            for b, part in enumerate(rows):
-                wide[zp, b * 3 * n : (b + 1) * 3 * n, cols] = part.astype(BF16)
+        below = where < HALF
+        for r in range(0, n, part):
+            xs, us = [], []
+            for tp in range(pairs + 2):
+                v = load(tp, slice(r, r + part))
+                left = jnp.where(column == 0, 0.0, pltpu.roll(v, 1, 1))
+                right = jnp.where(column == HALF - 1, 0.0, pltpu.roll(v, LANES - 1, 1))
+                xs.append((left, v, right))
+                us.append([pltpu.roll(x, HALF, 1) for x in xs[-1]])
+            for t in range(pairs):
+                cols = slice(t * LANES, (t + 1) * LANES)
+                for c in range(3):
+                    taps = (
+                        jnp.where(below, us[t][c], us[t + 1][c]),
+                        xs[t + 1][c],
+                        jnp.where(below, us[t + 1][c], us[t + 2][c]),
+                    )
+                    for b, tap in enumerate(taps):
+                        base = (3 * b + c) * n + r
+                        wide[zp, base : base + part, cols] = tap.astype(BF16)
 
     def coarse_conv(w, n, halo, act, layer, wide, store):
-        top = jnp.zeros((n, LANES), F32)
+        top = jnp.zeros((2 * 8, LANES), F32)
 
         def inner(zp):
-            def load(tp):
+            def load(tp, rows):
                 nonlocal top
                 if tp in (0, pairs + 1):
                     side = int(tp > 0)
                     bound = limit(layer, 0, 2 * side - 1)
-                    v = act(halo.yface[side, zp - 1])
+                    v = act(halo.yface[side, zp - 1, rows], rows)
                 else:
                     bound = bounds[layer]
-                    v = act(halo.src[zp - 1, tp - 1])
+                    v = act(halo.src[zp - 1, tp - 1, rows], rows)
                     top = jnp.maximum(top, jnp.abs(v))
                 return jnp.clip(v, -bound, bound)
 
             return load
 
         def outer(side):
-            def load(tp):
+            def load(tp, rows):
                 if tp in (0, pairs + 1):
                     other = int(tp > 0)
                     bound = limit(layer, 2 * side - 1, 2 * other - 1)
-                    v = act(halo.corner[side * 2 + other])
+                    v = act(halo.corner[side * 2 + other, rows], rows)
                 else:
                     bound = limit(layer, 2 * side - 1, 0)
-                    v = act(halo.zface[side, tp - 1])
+                    v = act(halo.zface[side, tp - 1, rows], rows)
                 return jnp.clip(v, -bound, bound)
 
             return load
@@ -465,7 +487,7 @@
     def blocks(mine):
         out = []
         for k in range(1, ny):
-            other = lax.rem(my_y + k, ny)
+            other = ys[k]
             at = my_y if mine else other
             out.append(remote(vals4.at[other], fin.at[at], fin_s.at[k], fin_r.at[at], {"sy": other}))
         return out
@@ -482,7 +504,7 @@
     peak_all[my_s, 0:1, :] = row
 
     def across(k, mine):
-        other = lax.rem(my_s + k, ns)
+        other = ahead(my_s, k, ns)
         slot = my_s if mine else other
         ref = peak_all.at[slot, pl.ds(0, 1)]
         return remote(ref, ref, pa_s.at[k], pa_r.at[slot], {"sample": other})
@@ -506,8 +528,7 @@
         across(k, False).wait_recv()
         across(k, True).wait_send()
     row = tree(jnp.maximum, [peak_all[i, 0:1, :] for i in range(ns)])
-    for i in range(4):
-        peak_out[i] = jnp.max(jnp.where(at == i, row, 0.0))
+    peak_out[...] = row[0, 0 : peak_out.shape[0]]
 
 
 def per_device(sizes, volume, hist, c1, c2, c3, c4, gf, sf, gc, sc):
@@ -521,6 +542,7 @@
     assert xc == LANES and zc % 2 == 0 and yc % 4 == 0 and wc <= HALF
 
     args = (volume[0], hist, c1, c2, c3, c4, gf, sf, gc, sc)
+    args = tuple(pltpu.with_memory_space_constraint(x, pltpu.HBM) for x in args)
     vmem = pl.BlockSpec(memory_space=pltpu.VMEM)
     dma = pltpu.SemaphoreType.DMA
 
@@ -539,7 +561,7 @@
             jax.ShapeDtypeStruct((4,), F32),
         ),
         in_specs=[pl.BlockSpec(memory_space=IN_SPACE)] * len(args),
-        out_specs=(vmem, vmem, pl.BlockSpec(memory_space=pltpu.SMEM)),
+        out_specs=(vmem, vmem, vmem),
         scratch_shapes=[
             *[pltpu.VMEM(a.shape, a.dtype) for a in args],
             pltpu.VMEM((3 * ch, 9 * ch), BF16),
@@ -583,26 +605,28 @@
         ),
     )(*args)
 
-    def finish(a, b, c, oa, ob, oc_):
-        oa[...] = a[...]
-        ob[...] = b[...]
-        for i in range(4):
-            oc_[i] = c[i]
-
-    smem = pl.BlockSpec(memory_space=pltpu.SMEM)
+    def finish(*refs):
+        copies = [pltpu.make_async_copy(refs[i], refs[3 + i], refs[6].at[i]) for i in range(3)]
+        for copy in copies:
+            copy.start()
+        for copy in copies:
+            copy.wait()
+
+    anywhere = pl.BlockSpec(memory_space=pl.ANY)
     skip, coarse, peaks = pl.pallas_call(
         finish,
         out_shape=tuple(jax.ShapeDtypeStruct(a.shape, a.dtype) for a in (skip, coarse, peaks)),
-        in_specs=[vmem, vmem, smem],
-        out_specs=(vmem, vmem, smem),
+        in_specs=[anywhere] * 3,
+        out_specs=[anywhere] * 3,
+        scratch_shapes=[dma((3,))],
         compiler_params=pltpu.CompilerParams(vmem_limit_bytes=FINISH_BYTES),
     )(skip, coarse, peaks)
     return skip[None], coarse[None], peaks
 
 
 IN_SPACE = pltpu.HBM
-VMEM_BYTES = 56 * 1024 * 1024
-FINISH_BYTES = 56 * 1024 * 1024
+VMEM_BYTES = 20 * 1024 * 1024
+FINISH_BYTES = 4 * 1024 * 1024
 
 
 def solution(mesh):

time: 38.1 us -> 35.3 us (0.927)
  Pallas kernels: 37.3 us -> 34.5 us
    pallas_call x1, Pallas kernels: 35.6 us -> 33.7 us  [per_device(): pl.pallas_call(functools.partial(network, sizes), out_shape=(jax.ShapeDty...]
    pallas_call x1, Pallas kernels: 1.71 us -> 0.75 us  [per_device(): pl.pallas_call(finish, out_shape=tuple((jax.ShapeDtypeStruct(a.shape, a.d...]
where the time goes in v2:
time: 35.3 us; the launch traced here: 35.1 us
  Pallas kernels  34.5 us (98%)
  between operations  0.64 us (2%)
    pallas_call x1, Pallas kernels, per_device(): pl.pallas_call(functools.partial(network, sizes), out_shape=(jax.ShapeDty...  33.7 us
    pallas_call x1, Pallas kernels, per_device(): pl.pallas_call(finish, out_shape=tuple((jax.ShapeDtypeStruct(a.shape, a.d...  0.75 us

profile of v2, /device:TPU:0, one launch (start us, length us, event | category | flops | bytes accessed | tf_op | source)
XLA Modules:
  0.0 35.1 jit_solution(6098288286247560207)
XLA Ops:
  0.6 33.7 %shard_map.121 = (bf16[32,4,8,128]{3,2,1,0:T(8,128)(2,1)S(1)}, bf16[16,2,1024]{2,1,0:T(2,128)(2,1)S(1)}, f32[4]{0:T(128)S(1)}) custom-call(bf16[32,4,8,128]{3,2,1,0:T(8,128)(2,1)} %bitcast.3, f32[4,16]{1,0:T(4,128)} %refs_1_.1, bf16[27,32,32]{2,1,0:T(8,128)(2,1)} %refs_2_.1, bf16[27,32,32]{2,1,0:T(8,128)(2,1)} %refs_3_.1, bf16[27,16,32]{2,1,0:T(8,128)(2,1)} %refs_4_.1, ...), custom_call_target="tpu_custom_call" | custom-call | tf_op jit(solution)/shard_map/pallas_call | solution.py:556
  34.4 0.7 %shard_map.122 = (bf16[32,4,8,128]{3,2,1,0:T(8,128)(2,1)}, bf16[16,2,1024]{2,1,0:T(2,128)(2,1)}, f32[4]{0:T(128)}) custom-call(bf16[32,4,8,128]{3,2,1,0:T(8,128)(2,1)S(1)} %get-tuple-element.9.refs_0_, bf16[16,2,1024]{2,1,0:T(2,128)(2,1)S(1)} %get-tuple-element.10.refs_1_, f32[4]{0:T(128)S(1)} %get-tuple-element.11.refs_2_), custom_call_target="tpu_custom_call" | custom-call | tf_op jit(solution)/shard_map/pallas_call | solution.py:616

commit v3 on v2

--- a/solution.py
+++ b/solution.py
@@ -76,8 +76,12 @@
         return jnp.where(index >= count, index - count, index)
 
     ys = [my_y] + [ahead(my_y, k, ny) for k in range(1, ny)]
-    zs = [my_z] + [ahead(my_z, k, nz) for k in range(1, nz)]
-    far = sorted(range(1, group), key=lambda k: -min(k % nz, -k % nz))
+    zs = [my_z]
+    for j in range(nz - 1):
+        down = nz - 1 - j
+        down = jnp.where(down > my_z, down, down - 1)
+        zs.append(jnp.where(2 * my_z < nz, down, jnp.where(j < my_z, j, j + 1)))
+    far = sorted(range(1, group), key=lambda k: (k % nz == 0, k % nz, -min(k // nz, -(k // nz) % ny)))
 
     def member(k):
         return {"sy": ys[k // nz], "sz": zs[k % nz]}
@@ -126,7 +130,7 @@
             return remote(src, self.landing(d), halo_s.at[at], halo_r.at[at], where)
 
         def start(self):
-            for d, (dz, dy) in enumerate(STEPS):
+            for d, (dz, dy) in sorted(enumerate(STEPS), key=lambda e: -abs(e[1][0] * e[1][1])):
                 @pl.when(inside(dz, dy))
                 def _():
                     self.copy(d).start()

time: 35.3 us -> 34.4 us (0.975)
  Pallas kernels: 34.5 us -> 33.6 us
    pallas_call x1, Pallas kernels: 33.7 us -> 32.8 us  [per_device(): pl.pallas_call(functools.partial(network, sizes), out_shape=(jax.ShapeDty...]
where the time goes in v3:
time: 34.4 us; the launch traced here: 34.2 us
  Pallas kernels  33.6 us (98%)
  between operations  0.64 us (2%)
    pallas_call x1, Pallas kernels, per_device(): pl.pallas_call(functools.partial(network, sizes), out_shape=(jax.ShapeDty...  32.8 us
    pallas_call x1, Pallas kernels, per_device(): pl.pallas_call(finish, out_shape=tuple((jax.ShapeDtypeStruct(a.shape, a.d...  0.75 us

profile of v3, /device:TPU:0, one launch (start us, length us, event | category | flops | bytes accessed | tf_op | source)
XLA Modules:
  0.0 34.2 jit_solution(14796443774711958396)
XLA Ops:
  0.6 32.8 %shard_map.121 = (bf16[32,4,8,128]{3,2,1,0:T(8,128)(2,1)S(1)}, bf16[16,2,1024]{2,1,0:T(2,128)(2,1)S(1)}, f32[4]{0:T(128)S(1)}) custom-call(bf16[32,4,8,128]{3,2,1,0:T(8,128)(2,1)} %bitcast.3, f32[4,16]{1,0:T(4,128)} %refs_1_.1, bf16[27,32,32]{2,1,0:T(8,128)(2,1)} %refs_2_.1, bf16[27,32,32]{2,1,0:T(8,128)(2,1)} %refs_3_.1, bf16[27,16,32]{2,1,0:T(8,128)(2,1)} %refs_4_.1, ...), custom_call_target="tpu_custom_call" | custom-call | tf_op jit(solution)/shard_map/pallas_call | solution.py:560
  33.5 0.7 %shard_map.122 = (bf16[32,4,8,128]{3,2,1,0:T(8,128)(2,1)}, bf16[16,2,1024]{2,1,0:T(2,128)(2,1)}, f32[4]{0:T(128)}) custom-call(bf16[32,4,8,128]{3,2,1,0:T(8,128)(2,1)S(1)} %get-tuple-element.9.refs_0_, bf16[16,2,1024]{2,1,0:T(2,128)(2,1)S(1)} %get-tuple-element.10.refs_1_, f32[4]{0:T(128)S(1)} %get-tuple-element.11.refs_2_), custom_call_target="tpu_custom_call" | custom-call | tf_op jit(solution)/shard_map/pallas_call | solution.py:620
